TPU v7x, 32 devices: a whole 2x2x4 slice. The times are simulated.
32 devices in a mesh: grp: 2 (over x), seq: 8 (over z, y), kv: 2 (over core).
Axes of the slice: x: 2, y: 2, z: 4, core: 2. Of those that a mesh axis runs over, the one named last changes fastest.
Arguments:
- queries: bfloat16 [4, 64, 128], P(('grp', 'kv'), 'seq'), parts along dimension 0, may hold values from -256 to 256
- keys: bfloat16 [4, 16384, 8, 128], P(('grp', 'kv'), 'seq'), parts along dimension 0, may hold values from -6 to 6
- values: bfloat16 [4, 16384, 8, 128], P(('grp', 'kv'), 'seq'), parts along dimension 0, may hold values from -6 to 6
- picks: int32 [4, 64, 3], P(('grp', 'kv'), 'seq'), parts along dimension 0, may hold values from 0 to 31, as said below
- lengths: int32 [4], P(('grp', 'kv')), parts along dimension 0, may hold values from 8194 to 16384, as said below
Outputs:
- attended: bfloat16 [4, 64, 128], P(('grp', 'kv'), 'seq'), parts along dimension 0
There are 2 independent parts, one for each index of `grp`. A program takes and returns all parts, laid end to end along the dimension named above; each array names one. Nothing has to cross between parts.
Inputs may be any that keep to these rules, and one draw needn't show every extreme that they name: `picks`: each row of 3 holds distinct block numbers in ascending order; the last is the block that holds position lengths[b] - 1, the others lie before it. Position lengths[b] - 1 is never the first position of its block.
All inputs are finite; a program needn't handle non-finite values.
Results may differ from a plain program's by a relative error of at most 0.0046.
Values may be sent and summed in bfloat16 or wider, within the bound.
A program may use at most 64 MiB of HBM per device.

v0:
```python
import math
import jax
import jax.numpy as jnp
from jax import lax
from jax.sharding import PartitionSpec as P

BLOCK = 512
NEGATIVE = -1e30


def shards(queries, keys, values, picks, lengths):
    rows = queries.shape[0]
    head_dim = queries.shape[2]
    local_len = keys.shape[1]
    kv_heads = keys.shape[2]
    blocks_here = local_len // BLOCK
    seq_index = lax.axis_index("seq")
    all_queries, all_picks = (
        lax.all_gather(queries, "seq", axis=1, tiled=True),
        lax.all_gather(picks, "seq", axis=1, tiled=True),
    )
    heads = all_queries.shape[1]
    group = heads // kv_heads
    grouped = all_queries.reshape(rows, kv_heads, group, head_dim)
    scores = jnp.einsum("bkgd,btkd->bkgt", grouped, keys, preferred_element_type=jnp.float32) * (
        1.0 / math.sqrt(head_dim)
    )
    scores = scores.reshape(rows, kv_heads, group, blocks_here, BLOCK)
    block_ids = seq_index * blocks_here + jnp.arange(blocks_here, dtype=jnp.int32)
    chosen = jnp.any(all_picks[:, :, :, None] == block_ids[None, None, None, :], axis=2)
    chosen = chosen.reshape(rows, kv_heads, group, blocks_here)
    positions = block_ids[:, None] * BLOCK + jnp.arange(BLOCK, dtype=jnp.int32)[None, :]
    inside = positions[None, :, :] < lengths[:, None, None]
    live = jnp.logical_and(chosen[..., None], inside[:, None, None, :, :])
    masked = jnp.where(live, scores, -jnp.inf)
    any_live = jnp.any(live, axis=-1)
    safe_max = jnp.where(any_live, jnp.max(masked, axis=-1), NEGATIVE)
    weight = jnp.exp(masked - safe_max[..., None])
    block_total = jnp.sum(weight, axis=-1)
    rounded = weight.astype(jnp.bfloat16)
    blocked_values = values.reshape(rows, blocks_here, BLOCK, kv_heads, head_dim)
    block_out = jnp.einsum(
        "bkgnt,bntkd->bkgnd", rounded, blocked_values, preferred_element_type=jnp.float32
    )
    device_max = jnp.max(safe_max, axis=-1)
    coef = jnp.exp(safe_max - device_max[..., None])
    partial_out = jnp.sum(block_out * coef[..., None], axis=3).reshape(rows, heads, head_dim)
    partial_total = jnp.sum(block_total * coef, axis=-1).reshape(rows, heads)
    partial_max = device_max.reshape(rows, heads)
    came_out, came_max, came_total = (
        lax.all_to_all(partial_out[None], "seq", split_axis=2, concat_axis=0, tiled=True),
        lax.all_to_all(partial_max[None], "seq", split_axis=2, concat_axis=0, tiled=True),
        lax.all_to_all(partial_total[None], "seq", split_axis=2, concat_axis=0, tiled=True),
    )
    top = jnp.max(came_max, axis=0)
    rescale = jnp.exp(came_max - top[None])
    mine_out = jnp.sum(came_out * rescale[..., None], axis=0)
    mine_total = jnp.sum(came_total * rescale, axis=0)
    return (mine_out / mine_total[..., None]).astype(jnp.bfloat16)


def solution(mesh):
    return jax.shard_map(
        shards,
        mesh=mesh,
        in_specs=(
            P(("grp", "kv"), "seq", None),
            P(("grp", "kv"), "seq", None, None),
            P(("grp", "kv"), "seq", None, None),
            P(("grp", "kv"), "seq", None),
            P(("grp", "kv")),
        ),
        out_specs=P(("grp", "kv"), "seq", None),
        check_vma=False,
    )
```

profile of v0, /device:TPU:0, one launch (start us, length us, event | category | flops | bytes accessed | tf_op | source)
XLA Modules:
  0.0 97.5 jit_solution(2691425866918644044)
XLA Ops:
  0.7 0.8 copy.28
  1.4 28.1 %all_gather.7 = bf16[1,64,128]{2,1,0:T(8,128)(2,1)S(1)} all-gather(bf16[1,8,128]{2,1,0:T(8,128)(2,1)} %param.5), channel_id=1, replica_groups=mesh['grp'=2,'seq'=8,'kv'=2] {'seq'}, dimensions={1}, use_global_device_ids=true | all-gather | bytes 18432 | tf_op jit(solution)/shard_map/all_gather | solution.py:19
  29.5 30.6 %all_gather.6 = s32[1,64,3]{2,0,1:T(1,128)S(1)} all-gather(s32[1,8,3]{2,0,1:T(1,128)S(1)} %copy.28), channel_id=1, replica_groups=mesh['grp'=2,'seq'=8,'kv'=2] {'seq'}, dimensions={1}, use_global_device_ids=true | all-gather | bytes 864 | tf_op jit(solution)/shard_map/all_gather | solution.py:20
  60.1 0.1 copy.29
  60.1 0.1 compare_reduce_fusion
  60.2 0.1 and.40
  60.3 0.1 add_compare_fusion
  60.4 0.7 and_reduce_fusion
  61.1 3.4 %fusion.4 = f32[8,8,2048]{2,1,0:T(8,128)S(1)} fusion(bf16[2048,8,128]{2,1,0:T(8,128)(2,1)} %bitcast.31, bf16[1,64,128]{2,1,0:T(8,128)(2,1)S(1)} %all_gather.7), kind=kOutput, calls=%fused_computation.4 | convolution fusion | flops 33685504 | bytes 4734976 | tf_op jit(solution)/shard_map/bkgd,btkd->bkgt/dot_general | solution.py:25
  64.5 0.2 fusion.16
  64.8 0.7 broadcast_in_dim_reshape.13
  65.5 3.9 %all-to-all-start.1 = ((f32[1,1,64]{1,0,2:T(1,128)}), f32[1,1,64]{1,0,2:T(1,128)S(1)}, u32[]{:S(2)}, u32[]{:S(2)}) async-start(f32[1,1,64]{1,0,2:T(1,128)} %broadcast_in_dim_reshape.13), calls=%async_computation.1 | async-start | bytes 65536 | tf_op jit(solution)/shard_map/all_to_all | solution.py:52
  69.4 0.3 exponential_reduce_fusion
  69.7 0.7 broadcast_in_dim_reshape.14
  70.4 5.6 %all-to-all-done.1 = f32[1,1,64]{1,0,2:T(1,128)S(1)} async-done(((f32[1,1,64]{1,0,2:T(1,128)}), f32[1,1,64]{1,0,2:T(1,128)S(1)}, u32[]{:S(2)}, u32[]{:S(2)}) %all-to-all-start.1) | async-done | bytes 288 | tf_op jit(solution)/shard_map/all_to_all | solution.py:52
  76.1 3.3 %all-to-all-start.2 = ((f32[1,1,64]{1,0,2:T(1,128)}), f32[1,1,64]{1,0,2:T(1,128)S(1)}, u32[]{:S(2)}, u32[]{:S(2)}) async-start(f32[1,1,64]{1,0,2:T(1,128)} %broadcast_in_dim_reshape.14), calls=%async_computation.2 | async-start | bytes 65536 | tf_op jit(solution)/shard_map/all_to_all | solution.py:53
  79.4 4.1 %fusion.13 = f32[8,8,128]{2,1,0:T(8,128)} fusion(bf16[4,512,8,128]{3,2,1,0:T(8,128)(2,1)} %bitcast.34, f32[8,8,4,512]{3,1,2,0:T(8,128)S(1)} %bitcast.30, f32[8,8,4]{1,2,0:T(4,128)S(1)} %get-tuple-element.8, pred[4,512]{1,0:T(4,128)(4,1)S(1)} %add_compare_fusion, pred[8,8,4]{1,2,0:T(4,128)(4,1)S(1)} %copy.30, f32[8,8,4]{1,2,0:T(4,128)S(1)} %get-tuple-element.6), kind=kOutput, calls=%fused_computation.7 | convolution fusion | flops 34136064 | bytes 4755712 | tf_op jit(solution)/shard_map/bkgnt,bntkd->bkgnd/dot_general | solution.py:42
  83.5 0.6 reduce.12
  84.0 0.1 all_to_all.32
  84.1 0.1 all_to_all.35
  84.2 1.9 %all-to-all-done.2 = f32[1,1,64]{1,0,2:T(1,128)S(1)} async-done(((f32[1,1,64]{1,0,2:T(1,128)}), f32[1,1,64]{1,0,2:T(1,128)S(1)}, u32[]{:S(2)}, u32[]{:S(2)}) %all-to-all-start.2) | async-done | bytes 288 | tf_op jit(solution)/shard_map/all_to_all | solution.py:53
  86.0 4.1 %all-to-all-start = ((f32[1,1,64,128]{3,1,0,2:T(1,128)}), f32[1,1,64,128]{3,1,0,2:T(1,128)S(1)}, u32[]{:S(2)}, u32[]{:S(2)}) async-start(f32[1,1,64,128]{3,1,0,2:T(1,128)} %bitcast.10), calls=%async_computation | async-start | bytes 65536 | tf_op jit(solution)/shard_map/all_to_all | solution.py:51
  90.1 0.6 reduce.13
  90.7 0.1 all_to_all.34
  90.8 6.0 %all-to-all-done = f32[1,1,64,128]{3,1,0,2:T(1,128)S(1)} async-done(((f32[1,1,64,128]{3,1,0,2:T(1,128)}), f32[1,1,64,128]{3,1,0,2:T(1,128)S(1)}, u32[]{:S(2)}, u32[]{:S(2)}) %all-to-all-start) | async-done | bytes 32800 | tf_op jit(solution)/shard_map/all_to_all | solution.py:51
  96.8 0.1 multiply_reduce_fusion
  96.9 0.7 fusion.22
  (8 shorter events, 0.1 us)
Async XLA Ops:
  65.5 10.5 %all-to-all-start.1 = ((f32[1,1,64]{1,0,2:T(1,128)}), f32[1,1,64]{1,0,2:T(1,128)S(1)}, u32[]{:S(2)}, u32[]{:S(2)}) async-start(f32[1,1,64]{1,0,2:T(1,128)} %broadcast_in_dim_reshape.13), calls=%async_computation.1 | async-start | bytes 65536 | tf_op jit(solution)/shard_map/all_to_all | solution.py:52
  76.1 10.0 %all-to-all-start.2 = ((f32[1,1,64]{1,0,2:T(1,128)}), f32[1,1,64]{1,0,2:T(1,128)S(1)}, u32[]{:S(2)}, u32[]{:S(2)}) async-start(f32[1,1,64]{1,0,2:T(1,128)} %broadcast_in_dim_reshape.14), calls=%async_computation.2 | async-start | bytes 65536 | tf_op jit(solution)/shard_map/all_to_all | solution.py:53
  86.0 10.8 %all-to-all-start = ((f32[1,1,64,128]{3,1,0,2:T(1,128)}), f32[1,1,64,128]{3,1,0,2:T(1,128)S(1)}, u32[]{:S(2)}, u32[]{:S(2)}) async-start(f32[1,1,64,128]{3,1,0,2:T(1,128)} %bitcast.10), calls=%async_computation | async-start | bytes 65536 | tf_op jit(solution)/shard_map/all_to_all | solution.py:51
where the time goes:
time: 98 us; the launch traced here: 97.5 us
  blocking collectives  58.7 us (60%)
  waiting for transfers between devices  13.5 us (14%)
  starting transfers between devices  11.3 us (12%)
  matrix products  7.44 us (8%)
  other arithmetic  3.38 us (3%)
  local copies, waits for them, and re-layouts  2.59 us (3%)
    all_gather x1, blocking collectives, shards(): lax.all_gather(picks, 'seq', axis=1, tiled=True)  30.6 us
    all_gather x1, blocking collectives, shards(): lax.all_gather(queries, 'seq', axis=1, tiled=True)  28.1 us
    all_to_all x1, waiting for transfers between devices, shards(): lax.all_to_all(partial_out[None], 'seq', split_axis=2, concat_axis=0, til...  5.99 us
    all_to_all x1, waiting for transfers between devices, shards(): lax.all_to_all(partial_max[None], 'seq', split_axis=2, concat_axis=0, til...  5.64 us
    all_to_all x1, starting transfers between devices, shards(): lax.all_to_all(partial_out[None], 'seq', split_axis=2, concat_axis=0, til...  4.09 us
    dot_general x1, matrix products, shards(): jnp.einsum('bkgnt,bntkd->bkgnd', rounded, blocked_values, preferred_eleme...  4.05 us
    all_to_all x1, starting transfers between devices, shards(): lax.all_to_all(partial_max[None], 'seq', split_axis=2, concat_axis=0, til...  3.86 us
    dot_general x1, matrix products, shards(): jnp.einsum('bkgd,btkd->bkgt', grouped, keys, preferred_element_type=jnp.f...  3.38 us
  transfers between devices with their start and end apart: 3, of which 3 were waited for; matrix products, arithmetic and copies ran while one was open for 6% of the time, Pallas kernels for 0%

commit v1 on v0

--- a/solution.py
+++ b/solution.py
@@ -17,7 +17,7 @@
     seq_index = lax.axis_index("seq")
     all_queries, all_picks = (
         lax.all_gather(queries, "seq", axis=1, tiled=True),
-        lax.all_gather(picks, "seq", axis=1, tiled=True),
+        jnp.concatenate(lax.all_gather(picks, "seq"), axis=1),
     )
     heads = all_queries.shape[1]
     group = heads // kv_heads

time: 98 us -> 92.8 us (0.947)
  blocking collectives: 58.7 us -> 54.2 us
    all_gather x1, blocking collectives: 30.6 us -> 27.9 us  [shards(): lax.all_gather(picks, 'seq')]
    all_gather x1, blocking collectives: 28.1 us -> 26.3 us  [shards(): lax.all_gather(queries, 'seq', axis=1, tiled=True)]
  transfers between devices with their start and end apart: 3 -> 3, of which waited for: 3 -> 3; matrix products, arithmetic and copies ran while one was open for 6% -> 7% of each run, Pallas kernels for 0% -> 0%
where the time goes in v1:
time: 92.8 us; the launch traced here: 92.4 us
  blocking collectives  54.2 us (58%)
  waiting for transfers between devices  13.4 us (14%)
  starting transfers between devices  10.8 us (12%)
  matrix products  7.44 us (8%)
  other arithmetic  3.38 us (4%)
  local copies, waits for them, and re-layouts  2.52 us (3%)
    all_gather x1, blocking collectives, shards(): lax.all_gather(picks, 'seq')  27.9 us
    all_gather x1, blocking collectives, shards(): lax.all_gather(queries, 'seq', axis=1, tiled=True)  26.3 us
    all_to_all x1, waiting for transfers between devices, shards(): lax.all_to_all(partial_out[None], 'seq', split_axis=2, concat_axis=0, til...  5.99 us
    all_to_all x1, waiting for transfers between devices, shards(): lax.all_to_all(partial_max[None], 'seq', split_axis=2, concat_axis=0, til...  5.57 us
    all_to_all x1, starting transfers between devices, shards(): lax.all_to_all(partial_out[None], 'seq', split_axis=2, concat_axis=0, til...  4.09 us
    dot_general x1, matrix products, shards(): jnp.einsum('bkgnt,bntkd->bkgnd', rounded, blocked_values, preferred_eleme...  4.05 us
    dot_general x1, matrix products, shards(): jnp.einsum('bkgd,btkd->bkgt', grouped, keys, preferred_element_type=jnp.f...  3.38 us
    all_to_all x1, starting transfers between devices, shards(): lax.all_to_all(partial_total[None], 'seq', split_axis=2, concat_axis=0, t...  3.33 us
  transfers between devices with their start and end apart: 3, of which 3 were waited for; matrix products, arithmetic and copies ran while one was open for 7% of the time, Pallas kernels for 0%

profile of v1, /device:TPU:0, one launch (start us, length us, event | category | flops | bytes accessed | tf_op | source)
XLA Modules:
  0.0 92.4 jit_solution(726402913111988964)
XLA Ops:
  0.7 0.7 copy.30
  1.3 27.9 %all-gather = s32[8,8,3]{1,2,0:T(4,128)S(1)} all-gather(s32[1,8,3]{1,2,0:T(4,128)S(1)} %copy.30), channel_id=2, replica_groups=mesh['grp'=2,'seq'=8,'kv'=2] {'seq'}, dimensions={0}, use_global_device_ids=true | all-gather | bytes 864 | tf_op jit(solution)/shard_map/all_gather | solution.py:20
  29.3 0.1 eq.23
  29.3 0.1 compare_reduce_fusion
  29.4 0.1 and.40
  29.5 26.3 %all_gather.11 = bf16[1,64,128]{2,1,0:T(8,128)(2,1)S(1)} all-gather(bf16[1,8,128]{2,1,0:T(8,128)(2,1)} %param.5), channel_id=1, replica_groups=mesh['grp'=2,'seq'=8,'kv'=2] {'seq'}, dimensions={1}, use_global_device_ids=true | all-gather | bytes 18432 | tf_op jit(solution)/shard_map/all_gather | solution.py:19
  55.8 0.1 add_compare_fusion
  55.9 0.7 and_reduce_fusion
  56.6 3.4 %fusion.4 = f32[8,8,2048]{2,1,0:T(8,128)S(1)} fusion(bf16[2048,8,128]{2,1,0:T(8,128)(2,1)} %bitcast.32, bf16[1,64,128]{2,1,0:T(8,128)(2,1)S(1)} %all_gather.11), kind=kOutput, calls=%fused_computation.4 | convolution fusion | flops 33685504 | bytes 4734976 | tf_op jit(solution)/shard_map/bkgd,btkd->bkgt/dot_general | solution.py:25
  60.0 0.2 fusion.16
  60.2 0.7 broadcast_in_dim_reshape.14
  61.0 3.3 %all-to-all-start.1 = ((f32[1,1,64]{1,0,2:T(1,128)}), f32[1,1,64]{1,0,2:T(1,128)S(1)}, u32[]{:S(2)}, u32[]{:S(2)}) async-start(f32[1,1,64]{1,0,2:T(1,128)} %broadcast_in_dim_reshape.14), calls=%async_computation.1 | async-start | bytes 65536 | tf_op jit(solution)/shard_map/all_to_all | solution.py:52
  64.3 0.3 exponential_reduce_fusion
  64.6 0.7 broadcast_in_dim_reshape.15
  65.3 5.6 %all-to-all-done.1 = f32[1,1,64]{1,0,2:T(1,128)S(1)} async-done(((f32[1,1,64]{1,0,2:T(1,128)}), f32[1,1,64]{1,0,2:T(1,128)S(1)}, u32[]{:S(2)}, u32[]{:S(2)}) %all-to-all-start.1) | async-done | bytes 288 | tf_op jit(solution)/shard_map/all_to_all | solution.py:52
  70.9 3.3 %all-to-all-start.2 = ((f32[1,1,64]{1,0,2:T(1,128)}), f32[1,1,64]{1,0,2:T(1,128)S(1)}, u32[]{:S(2)}, u32[]{:S(2)}) async-start(f32[1,1,64]{1,0,2:T(1,128)} %broadcast_in_dim_reshape.15), calls=%async_computation.2 | async-start | bytes 65536 | tf_op jit(solution)/shard_map/all_to_all | solution.py:53
  74.3 4.1 %fusion.13 = f32[8,8,128]{2,1,0:T(8,128)} fusion(bf16[4,512,8,128]{3,2,1,0:T(8,128)(2,1)} %bitcast.34, f32[8,8,4,512]{3,1,2,0:T(8,128)S(1)} %bitcast.31, f32[8,8,4]{1,2,0:T(4,128)S(1)} %get-tuple-element.8, pred[4,512]{1,0:T(4,128)(4,1)S(1)} %add_compare_fusion, pred[8,8,4]{1,2,0:T(4,128)(4,1)S(1)} %copy.32, f32[8,8,4]{1,2,0:T(4,128)S(1)} %get-tuple-element.6), kind=kOutput, calls=%fused_computation.7 | convolution fusion | flops 34136064 | bytes 4755712 | tf_op jit(solution)/shard_map/bkgnt,bntkd->bkgnd/dot_general | solution.py:42
  78.3 0.6 reduce.12
  78.9 0.1 all_to_all.32
  78.9 0.1 all_to_all.35
  79.0 1.9 %all-to-all-done.2 = f32[1,1,64]{1,0,2:T(1,128)S(1)} async-done(((f32[1,1,64]{1,0,2:T(1,128)}), f32[1,1,64]{1,0,2:T(1,128)S(1)}, u32[]{:S(2)}, u32[]{:S(2)}) %all-to-all-start.2) | async-done | bytes 288 | tf_op jit(solution)/shard_map/all_to_all | solution.py:53
  80.9 4.1 %all-to-all-start = ((f32[1,1,64,128]{3,1,0,2:T(1,128)}), f32[1,1,64,128]{3,1,0,2:T(1,128)S(1)}, u32[]{:S(2)}, u32[]{:S(2)}) async-start(f32[1,1,64,128]{3,1,0,2:T(1,128)} %bitcast.9), calls=%async_computation | async-start | bytes 65536 | tf_op jit(solution)/shard_map/all_to_all | solution.py:51
  85.0 0.6 reduce.13
  85.5 0.1 all_to_all.34
  85.7 6.0 %all-to-all-done = f32[1,1,64,128]{3,1,0,2:T(1,128)S(1)} async-done(((f32[1,1,64,128]{3,1,0,2:T(1,128)}), f32[1,1,64,128]{3,1,0,2:T(1,128)S(1)}, u32[]{:S(2)}, u32[]{:S(2)}) %all-to-all-start) | async-done | bytes 32800 | tf_op jit(solution)/shard_map/all_to_all | solution.py:51
  91.7 0.1 multiply_reduce_fusion
  91.7 0.7 fusion.22
  (9 shorter events, 0.1 us)
Async XLA Ops:
  61.0 10.0 %all-to-all-start.1 = ((f32[1,1,64]{1,0,2:T(1,128)}), f32[1,1,64]{1,0,2:T(1,128)S(1)}, u32[]{:S(2)}, u32[]{:S(2)}) async-start(f32[1,1,64]{1,0,2:T(1,128)} %broadcast_in_dim_reshape.14), calls=%async_computation.1 | async-start | bytes 65536 | tf_op jit(solution)/shard_map/all_to_all | solution.py:52
  70.9 10.0 %all-to-all-start.2 = ((f32[1,1,64]{1,0,2:T(1,128)}), f32[1,1,64]{1,0,2:T(1,128)S(1)}, u32[]{:S(2)}, u32[]{:S(2)}) async-start(f32[1,1,64]{1,0,2:T(1,128)} %broadcast_in_dim_reshape.15), calls=%async_computation.2 | async-start | bytes 65536 | tf_op jit(solution)/shard_map/all_to_all | solution.py:53
  80.9 10.8 %all-to-all-start = ((f32[1,1,64,128]{3,1,0,2:T(1,128)}), f32[1,1,64,128]{3,1,0,2:T(1,128)S(1)}, u32[]{:S(2)}, u32[]{:S(2)}) async-start(f32[1,1,64,128]{3,1,0,2:T(1,128)} %bitcast.9), calls=%async_computation | async-start | bytes 65536 | tf_op jit(solution)/shard_map/all_to_all | solution.py:51
